TPU v7x, 256 devices: a whole 4x4x8 slice. The times are simulated.
256 devices in a mesh: gx: 32 (over y, z_hi, core), ta: 8 (over x, z_lo).
Axes of the slice: x: 4, y: 4, z: 8 (z_hi: 4, z_lo: 2; z = z_hi * 2 + z_lo), core: 2. Of those that a mesh axis runs over, the one named last changes fastest.
Arguments:
- source: float32 [128, 1024, 512], P('ta', 'gx'), may hold values from -6 to 6
- previous: float32 [128, 1024, 512], P('ta', 'gx'), may hold values from -6 to 6
- time_modes: float32 [128, 128], replicated, as said below
- time_back: float32 [128, 128], replicated, as said below
- step_code: int32 [128], P('ta'), may hold values from 0 to 32
Outputs:
- next_iterate: float32 [128, 1024, 512], P('ta', 'gx')
Inputs may be any that keep to these rules, and one draw needn't show every extreme that they name: time_modes times time_back is the identity up to rounding. time_back is the inverse of time_modes up to rounding.
All inputs are finite; a program needn't handle non-finite values.
Results may differ from a plain program's by a relative error of at most 0.0001.
Values sent between devices are 32-bit elements; how exact they have to be, the bound alone decides.
No kernel may reach another device: no remote copies, remote signals or barrier semaphores. Data moves between devices by JAX's collectives and lax.ppermute only.
A program may use at most 64 MiB of HBM per device.

v0:
```python
import jax
import jax.numpy as jnp
from jax import lax
from jax.sharding import PartitionSpec as P

CY = 64
CZ = 8
CYCLES = 2
LEVELS = 3


ROBIN = 1.0
DAMPING = 0.8


def extended(block, sides, width):
    for axis, dim in sides:
        count = lax.axis_size(axis)
        forward = [(i, i + 1) for i in range(count - 1)]
        backward = [(target, source) for source, target in forward]
        low = lax.ppermute(
            lax.slice_in_dim(block, block.shape[dim] - width, None, axis=dim), axis, forward
        )
        high = lax.ppermute(lax.slice_in_dim(block, 0, width, axis=dim), axis, backward)
        block = jnp.concatenate([low, block, high], axis=dim)
    return block


def split_up(value, dim, length):
    before, after = (value.shape[:dim], value.shape[dim + 1 :])
    return jnp.moveaxis(value.reshape(*before, length, -1, *after), dim, 0)


def piece_ends(length, count):
    step = length // count
    if step >= 8:
        step -= step % 8
    return [step * k for k in range(1, count)]


def laid_out(tiles, dim):
    tiles = jnp.moveaxis(tiles, 0, dim)
    lengths = tiles.shape
    return tiles.reshape(*lengths[:dim], lengths[dim] * lengths[dim + 1], *lengths[dim + 2 :])


def several_exchanges(value, axis, pieces, split_dim, concat_dim):
    tiles = split_up(value, split_dim, lax.axis_size(axis))
    widest = max(range(1, max(2, tiles.ndim - 1)), key=lambda d: tiles.shape[d])
    done = []
    for section in jnp.split(tiles, piece_ends(tiles.shape[widest], pieces), axis=widest):
        if section.size:
            done.append(lax.all_to_all(section, axis, split_axis=0, concat_axis=0, tiled=True))
    return laid_out(jnp.concatenate(done, axis=widest), concat_dim)


def neighbour_sum(field, zdim, ydim):
    rank = field.ndim
    xpad = jnp.pad(field, [(0, 0)] * (rank - 2) + [(1, 1), (0, 0)])
    total = xpad[..., 2:, :] + xpad[..., :-2, :]
    zpad = jnp.pad(field, [(0, 0)] * (rank - 1) + [(ydim, ydim)])
    total = total + zpad[..., 2 * ydim :] + zpad[..., : -2 * ydim]
    ypad = jnp.pad(field, [(0, 0)] * (rank - 1) + [(1, 1)])
    column = jnp.arange(zdim * ydim) % ydim
    upper = (column != ydim - 1).astype(jnp.float32)
    lower = (column != 0).astype(jnp.float32)
    return total + upper * ypad[..., 2:] + lower * ypad[..., :-2]


def edge_weights(xdim, left, right):
    position = jnp.arange(xdim)[:, None]
    return left * (position == 0).astype(jnp.float32) + right * (position == xdim - 1).astype(
        jnp.float32
    )


def smooth(field, target, diag, scale, zdim, ydim, sweeps):
    for sweep in range(sweeps):
        applied = diag * field - scale * neighbour_sum(field, zdim, ydim)
        field = field + DAMPING * (target - applied) / diag
    return field


def plane_table(zdim, ydim):
    cells = jnp.arange(zdim * ydim)
    coarse_index = cells // ydim // 2 * (ydim // 2) + cells % ydim // 2
    targets = jnp.arange(zdim // 2 * (ydim // 2))
    return (coarse_index[:, None] == targets[None, :]).astype(jnp.float32)


def restrict(field, zdim, ydim):
    modes, groups, xdim, plane = field.shape
    paired = jnp.sum(field.reshape(modes, groups, xdim // 2, 2, plane), axis=3)
    table = plane_table(zdim, ydim) * 0.125
    return jnp.einsum("mgxc,cd->mgxd", paired, table, precision=lax.Precision.HIGHEST)


def prolong(field, zdim, ydim):
    modes, groups, xdim, plane = field.shape
    table = plane_table(zdim, ydim)
    spread = jnp.einsum("mgxd,cd->mgxc", field, table, precision=lax.Precision.HIGHEST)
    spread = jnp.broadcast_to(spread[:, :, :, None, :], (modes, groups, xdim, 2, zdim * ydim))
    return spread.reshape(modes, groups, 2 * xdim, zdim * ydim)


def vcycle(field, target, shifts, left, right, level, zdim, ydim):
    scale = 0.25**level
    edge = edge_weights(field.shape[2], left, right)
    diag = shifts + scale * (6.0 + edge)
    if level == LEVELS - 1:
        return smooth(field, target, diag, scale, zdim, ydim, 6)
    field = smooth(field, target, diag, scale, zdim, ydim, 2)
    resid = target - (diag * field - scale * neighbour_sum(field, zdim, ydim))
    coarse_target = restrict(resid, zdim, ydim)
    coarse = vcycle(
        jnp.zeros_like(coarse_target),
        coarse_target,
        shifts,
        left,
        right,
        level + 1,
        zdim // 2,
        ydim // 2,
    )
    field = field + prolong(coarse, zdim, ydim)
    return smooth(field, target, diag, scale, zdim, ydim, 2)


def solve_modes(target, shifts, left, right):
    field = jnp.zeros_like(target)
    for cycle in range(CYCLES):
        field = vcycle(field, target, shifts, left, right, 0, CZ, CY)
    return field


def body(source, previous, time_modes, time_back, step_code):
    block_steps = source.shape[0]
    group_index = lax.axis_index("gx")
    group_count = lax.axis_size("gx")
    has_left = (group_index > 0).astype(jnp.float32)
    has_right = (group_index < group_count - 1).astype(jnp.float32)
    padded = extended(previous, (("gx", 1),), 1)
    trace_left = has_left * (padded[:, 0, :] - ROBIN * previous[:, 0, :])
    trace_right = has_right * (padded[:, -1, :] - ROBIN * previous[:, -1, :])
    rhs = source.at[:, 0, :].add(trace_left).at[:, -1, :].add(trace_right)
    mixed = jnp.einsum(
        "mt,txc->mxc",
        time_modes,
        lax.all_to_all(rhs, "ta", split_axis=2, concat_axis=0, tiled=True),
        precision=lax.Precision.HIGHEST,
    )
    modes = several_exchanges(mixed, "ta", 2, 0, 2)
    shifts = (0.05 * jnp.exp2(step_code.astype(jnp.float32) / 4.0)).reshape(block_steps, 1, 1, 1)
    left = (ROBIN * has_left).reshape(1, 1, 1, 1)
    right = (ROBIN * has_right).reshape(1, 1, 1, 1)
    solved = solve_modes(modes[:, None], shifts, left, right)[:, 0]
    mixed = jnp.einsum(
        "tm,mxc->txc",
        time_back,
        lax.all_to_all(solved, "ta", split_axis=2, concat_axis=0, tiled=True),
        precision=lax.Precision.HIGHEST,
    )
    return lax.all_to_all(mixed, "ta", split_axis=0, concat_axis=2, tiled=True)


def solution(mesh):
    placed = (P("ta", "gx", None), P("ta", "gx", None), P(), P(), P("ta"))
    return jax.shard_map(
        body, mesh=mesh, in_specs=placed, out_specs=P("ta", "gx", None), check_vma=False
    )
```

profile of v0, /device:TPU:16, one launch (start us, length us, event | category | flops | bytes accessed | tf_op | source)
XLA Modules:
  0.0 202.9 jit_solution(14691321799922452808)
XLA Ops:
  4.9 5.3 %collective-permute-done = f32[16,1,512]{2,0,1:T(8,128)S(1)} collective-permute-done((f32[16,1,512]{2,0,1:T(8,128)S(1)}, f32[16,1,512]{2,0,1:T(8,128)S(1)}, u32[]{:S(2)}, u32[]{:S(2)}) %collective-permute-start) | collective-permute-done | bytes 32800 | tf_op jit(solution)/shard_map/ppermute | solution.py:21
  14.1 3.8 %copy.45 = f32[16,32,512]{1,0,2:T(8,128)} copy(f32[16,32,512]{2,0,1:T(8,128)S(1)} %fusion.389) | data formatting | bytes 2097152 | tf_op jit(solution)/shard_map/scatter-add | solution.py:145
  17.9 3.9 %reshape.561 = f32[8,1,32768]{2,1,0:T(1,128)S(1)} reshape(f32[512,16,32]{2,1,0:T(8,128)} %bitcast.97) | data formatting | bytes 2097152
  21.8 22.1 %all_to_all.64 = f32[8,1,32768]{2,1,0:T(1,128)S(1)} all-to-all(f32[8,1,32768]{2,1,0:T(1,128)S(1)} %reshape.561), channel_id=1, replica_groups=mesh['gx'=32,'ta'=8] {'ta'}, dimensions={0} | all-to-all | bytes 2097152 | tf_op jit(solution)/shard_map/all_to_all | solution.py:149
  44.4 3.1 %reduce.8 = f32[8,32768]{1,0:T(8,128)S(1)} reduce(f32[8,1,32768]{2,1,0:T(1,128)S(1)} %all_to_all.64, f32[]{:T(128)} %broadcast.1140), dimensions={1}, to_apply=%all_to_all.45.reduce_sub_computation | reduce | bytes 2097156 | tf_op jit(solution)/shard_map/all_to_all | solution.py:149
  47.5 3.3 %reshape.562 = f32[512,16,32]{2,1,0:T(8,128)} reshape(f32[8,32768]{1,0:T(8,128)S(1)} %reduce.8) | data formatting | bytes 2097152
  50.8 3.1 %copy.46 = f32[16,32,8,64]{3,1,0,2:T(8,128)S(1)} copy(f32[16,32,8,64]{1,0,3,2:T(8,128)} %bitcast.98) | data formatting | bytes 2097152 | tf_op jit(solution)/shard_map/all_to_all | solution.py:149
  53.9 4.1 %fusion.4 = f32[128,32,64]{0,2,1:T(8,128)S(1)} fusion(f32[128,32,64]{2,1,0:T(8,128)S(1)} %bitcast.101, f32[128,128]{1,0:T(8,128)S(1)} %copy-done), kind=kOutput, calls=%fused_computation.11 | convolution fusion | flops 402653184 | bytes 2162688 | tf_op jit(solution)/shard_map/mt,txc->mxc/dot_general | solution.py:146
  61.1 2.7 %reshape.565 = f32[8,1,16384]{2,1,0:T(1,128)} reshape(f32[8,16,16,64]{3,2,1,0:T(8,128)} %get-tuple-element.29) | data formatting | bytes 1048576
  63.8 3.5 %all-to-all-start.1 = ((f32[8,1,16384]{2,1,0:T(1,128)}), f32[8,1,16384]{2,1,0:T(1,128)S(1)}, u32[]{:S(2)}, u32[]{:S(2)}) async-start(f32[8,1,16384]{2,1,0:T(1,128)} %reshape.565), calls=%async_computation.1 | async-start | bytes 1048576 | tf_op jit(solution)/shard_map/all_to_all | solution.py:53
  68.8 9.0 %all-to-all-done.1 = f32[8,1,16384]{2,1,0:T(1,128)S(1)} async-done(((f32[8,1,16384]{2,1,0:T(1,128)}), f32[8,1,16384]{2,1,0:T(1,128)S(1)}, u32[]{:S(2)}, u32[]{:S(2)}) %all-to-all-start.1) | async-done | bytes 524320 | tf_op jit(solution)/shard_map/all_to_all | solution.py:53
  77.9 4.0 %all-to-all-start.2 = ((f32[8,1,16384]{2,1,0:T(1,128)}), f32[8,1,16384]{2,1,0:T(1,128)S(1)}, u32[]{:S(2)}, u32[]{:S(2)}) async-start(f32[8,1,16384]{2,1,0:T(1,128)} %reshape.563), calls=%async_computation.2 | async-start | bytes 1048576 | tf_op jit(solution)/shard_map/all_to_all | solution.py:53
  84.4 6.4 %all-to-all-done.2 = f32[8,1,16384]{2,1,0:T(1,128)S(1)} async-done(((f32[8,1,16384]{2,1,0:T(1,128)}), f32[8,1,16384]{2,1,0:T(1,128)S(1)}, u32[]{:S(2)}, u32[]{:S(2)}) %all-to-all-start.2) | async-done | bytes 524320 | tf_op jit(solution)/shard_map/all_to_all | solution.py:53
  134.7 3.7 %copy.50 = f32[16,32,512]{1,0,2:T(8,128)} copy(f32[16,32,512]{2,1,0:T(8,128)S(1)} %fusion.123) | data formatting | bytes 2097152 | tf_op jit(solution)/shard_map/squeeze | solution.py:156
  138.4 3.9 %reshape.567 = f32[8,1,32768]{2,1,0:T(1,128)S(1)} reshape(f32[512,16,32]{2,1,0:T(8,128)} %bitcast.99) | data formatting | bytes 2097152
  142.3 17.5 %all_to_all.65 = f32[8,1,32768]{2,1,0:T(1,128)S(1)} all-to-all(f32[8,1,32768]{2,1,0:T(1,128)S(1)} %reshape.567), channel_id=1, replica_groups=mesh['gx'=32,'ta'=8] {'ta'}, dimensions={0} | all-to-all | bytes 2097152 | tf_op jit(solution)/shard_map/all_to_all | solution.py:160
  159.8 3.1 %reduce.11 = f32[8,32768]{1,0:T(8,128)S(1)} reduce(f32[8,1,32768]{2,1,0:T(1,128)S(1)} %all_to_all.65, f32[]{:T(128)} %broadcast.1140), dimensions={1}, to_apply=%all_to_all.51.reduce_sub_computation | reduce | bytes 2097156 | tf_op jit(solution)/shard_map/all_to_all | solution.py:160
  163.0 3.3 %reshape.568 = f32[512,16,32]{2,1,0:T(8,128)} reshape(f32[8,32768]{1,0:T(8,128)S(1)} %reduce.11) | data formatting | bytes 2097152
  166.3 3.1 %copy.52 = f32[8,16,32,64]{3,2,1,0:T(8,128)S(1)} copy(f32[8,16,32,64]{2,1,3,0:T(8,128)} %bitcast.100) | data formatting | bytes 2097152 | tf_op jit(solution)/shard_map/all_to_all | solution.py:160
  169.4 4.1 %fusion.7 = f32[128,32,64]{0,2,1:T(8,128)S(1)} fusion(f32[128,32,64]{2,1,0:T(8,128)S(1)} %bitcast.102, f32[128,128]{1,0:T(8,128)S(1)} %copy-done.2), kind=kOutput, calls=%fused_computation.12 | convolution fusion | flops 402653184 | bytes 2162688 | tf_op jit(solution)/shard_map/tm,mxc->txc/dot_general | solution.py:157
  176.7 16.3 %all_to_all.66 = f32[8,1,32768]{2,1,0:T(1,128)S(1)} all-to-all(f32[8,1,32768]{2,1,0:T(1,128)S(1)} %reshape.569), channel_id=1, replica_groups=mesh['gx'=32,'ta'=8] {'ta'}, dimensions={0} | all-to-all | bytes 2097152 | tf_op jit(solution)/shard_map/all_to_all | solution.py:163
  193.0 3.1 %reduce.12 = f32[8,32768]{1,0:T(8,128)S(1)} reduce(f32[8,1,32768]{2,1,0:T(1,128)S(1)} %all_to_all.66, f32[]{:T(128)} %broadcast.1140), dimensions={1}, to_apply=%all_to_all.55.reduce_sub_computation | reduce | bytes 2097156 | tf_op jit(solution)/shard_map/all_to_all | solution.py:163
  197.0 3.0 %copy.55 = f32[16,32,8,64]{3,2,1,0:T(8,128)} copy(f32[16,32,8,64]{3,1,0,2:T(8,128)S(1)} %bitcast.104) | data formatting | bytes 2097152 | tf_op jit(solution)/shard_map/all_to_all | solution.py:163
  200.0 2.7 %all_to_all.58 = f32[16,32,512]{2,1,0:T(8,128)} reshape(f32[16,32,8,64]{3,2,1,0:T(8,128)} %copy.55) | data formatting | bytes 2097152 | tf_op jit(solution)/shard_map/all_to_all | solution.py:163
  (93 shorter events, 63.9 us)
Async XLA Ops:
  0.0 53.9 %copy-start = (f32[128,128]{1,0:T(8,128)S(1)}, f32[128,128]{1,0:T(8,128)}, u32[]{:S(2)}) copy-start(f32[128,128]{1,0:T(8,128)} %param.11) | copy-start | bytes 196612
  1.1 9.1 %collective-permute-start = (f32[16,1,512]{2,0,1:T(8,128)S(1)}, f32[16,1,512]{2,0,1:T(8,128)S(1)}, u32[]{:S(2)}, u32[]{:S(2)}) collective-permute-start(f32[16,1,512]{2,0,1:T(8,128)S(1)} %copy.58), channel_id=1, source_target_pairs={{0,8},{8,16},{16,24},{24,32},{32,40},{40,48},{48,56},{56,64},{64,7... | collective-permute-start | bytes 98312 | tf_op jit(solution)/shard_map/ppermute | solution.py:21
  10.3 3.8 %collective-permute-start.1 = (f32[16,1,512]{2,0,1:T(8,128)S(1)}, f32[16,1,512]{2,0,1:T(8,128)S(1)}, u32[]{:S(2)}, u32[]{:S(2)}) collective-permute-start(f32[16,1,512]{2,0,1:T(8,128)S(1)} %get-tuple-element.33), channel_id=1, source_target_pairs={{8,0},{16,8},{24,16},{32,24},{40,32},{48,40},{56,48},{64,56},{72,6... | collective-permute-start | bytes 98312 | tf_op jit(solution)/shard_map/ppermute | solution.py:24
  63.8 14.1 %all-to-all-start.1 = ((f32[8,1,16384]{2,1,0:T(1,128)}), f32[8,1,16384]{2,1,0:T(1,128)S(1)}, u32[]{:S(2)}, u32[]{:S(2)}) async-start(f32[8,1,16384]{2,1,0:T(1,128)} %reshape.565), calls=%async_computation.1 | async-start | bytes 1048576 | tf_op jit(solution)/shard_map/all_to_all | solution.py:53
  67.4 14.5 %copy-start.3 = (s32[16]{0:T(128)S(1)}, s32[16]{0:T(128)}, u32[]{:S(2)}) copy-start(s32[16]{0:T(128)} %param.13) | copy-start | bytes 196
  77.9 12.9 %all-to-all-start.2 = ((f32[8,1,16384]{2,1,0:T(1,128)}), f32[8,1,16384]{2,1,0:T(1,128)S(1)}, u32[]{:S(2)}, u32[]{:S(2)}) async-start(f32[8,1,16384]{2,1,0:T(1,128)} %reshape.563), calls=%async_computation.2 | async-start | bytes 1048576 | tf_op jit(solution)/shard_map/all_to_all | solution.py:53
  166.3 3.1 %copy-start.2 = (f32[128,128]{1,0:T(8,128)S(1)}, f32[128,128]{1,0:T(8,128)}, u32[]{:S(2)}) copy-start(f32[128,128]{1,0:T(8,128)} %param.12) | copy-start | bytes 196612
  197.0 5.7 %copy-start.1 = (f32[128,128]{1,0:T(8,128)S(1)}, f32[128,128]{1,0:T(8,128)}, u32[]{:S(2)}) copy-start(f32[128,128]{1,0:T(8,128)} %param.11) | copy-start | bytes 196612
where the time goes:
time: 206 us; the launch traced here: 203 us
  local copies, waits for them, and re-layouts  61.8 us (30%)
  blocking collectives  55.9 us (27%)
  other arithmetic  36.3 us (18%)
  waiting for transfers between devices  22.3 us (11%)
  matrix products  14 us (7%)
  starting transfers between devices  11.6 us (6%)
    unnamed x20, local copies, waits for them, and re-layouts  23.4 us
    all_to_all x1, blocking collectives, body(): lax.all_to_all(rhs, 'ta', split_axis=2, concat_axis=0, tiled=True)  22.1 us
    all_to_all x1, blocking collectives, body(): lax.all_to_all(solved, 'ta', split_axis=2, concat_axis=0, tiled=True)  17.5 us
    all_to_all x1, blocking collectives, body(): return lax.all_to_all(mixed, 'ta', split_axis=0, concat_axis=2, tiled=True)  16.3 us
    all_to_all x2, waiting for transfers between devices, several_exchanges(): lax.all_to_all(section, axis, split_axis=0, concat_axis=0, tiled=True)  15.4 us
    add x18, other arithmetic, smooth(): field = field + DAMPING * (target - applied) / diag  9.94 us
    all_to_all x2, starting transfers between devices, several_exchanges(): lax.all_to_all(section, axis, split_axis=0, concat_axis=0, tiled=True)  7.51 us
    broadcast_in_dim x6, local copies, waits for them, and re-layouts, prolong(): jnp.broadcast_to(spread[:, :, :, None, :], (modes, groups, xdim, 2, zdim...  6.65 us
  transfers between devices with their start and end apart: 4, of which 4 were waited for; matrix products, arithmetic and copies ran while one was open for 3% of the time, Pallas kernels for 0%

commit v1 on v0

v1 whole, which is shorter than its diff:
```python
import functools

import jax
import jax.numpy as jnp
from jax import lax
from jax.experimental import pallas as pl
from jax.experimental.pallas import tpu as pltpu
from jax.sharding import PartitionSpec as P

CYCLES = 2
ROBIN = 1.0
DAMPING = 0.8
LANES = 128
PLANES = 32
TILES = 4
UNROLL = 4

CHUNKS = ((0, 16),)
DEPTH = PLANES // (2 * len(CHUNKS))


def pack_kernel(starts, edges, *refs):
    if edges:
        source_ref, low_ref, high_ref, first_ref, last_ref, out_ref = refs
    else:
        source_ref, out_ref = refs
    steps = source_ref.shape[0]
    for i, start in enumerate(starts):
        for tile in range(TILES):
            peer = i * TILES + tile
            cells = pl.ds(tile * LANES, LANES)
            for t in range(steps):
                for row in range(0, DEPTH, 8):
                    out_ref[pl.ds((peer * DEPTH + row) * steps + t, 8, stride=steps), :] = source_ref[
                        t, pl.ds(start + row, 8), cells
                    ]
    if edges:
        group = lax.axis_index("gx")
        left = (group > 0).astype(jnp.float32)
        right = (group < lax.axis_size("gx") - 1).astype(jnp.float32)
        for i, start in enumerate(starts):
            for tile in range(TILES):
                cells = pl.ds(tile * LANES, LANES)
                peer = i * TILES + tile
                if start == 0:
                    rows = pl.ds(peer * DEPTH * steps, steps)
                    out_ref[rows, :] += left * (low_ref[:, cells] - ROBIN * first_ref[:, cells])
                if start + DEPTH == PLANES:
                    rows = pl.ds((peer * DEPTH + DEPTH - 1) * steps, steps)
                    out_ref[rows, :] += right * (high_ref[:, cells] - ROBIN * last_ref[:, cells])


def unpack_kernel(*refs):
    *in_refs, out_ref = refs
    steps = out_ref.shape[0]
    for starts, in_ref in zip(CHUNKS, in_refs):
        for i, start in enumerate(starts):
            for tile in range(TILES):
                peer = i * TILES + tile
                for t in range(steps):
                    for row in range(0, DEPTH, 8):
                        out_ref[t, pl.ds(start + row, 8), pl.ds(tile * LANES, LANES)] = in_ref[
                            pl.ds((peer * DEPTH + row) * steps + t, 8, stride=steps), :
                        ]


def halves(value):
    high = value.astype(jnp.bfloat16)
    return high, (value - high.astype(jnp.float32)).astype(jnp.bfloat16)


def product_kernel(matrix_ref, in_ref, out_ref):
    size = matrix_ref.shape[0]
    high, low = halves(matrix_ref[...])
    left = jnp.concatenate(
        [jnp.concatenate([high, high], axis=1), jnp.concatenate([low, low], axis=1)], axis=0
    )
    block = in_ref.shape[2]
    for x in range(0, DEPTH, 2):
        right = jnp.concatenate(
            [in_ref[:, x + k].reshape(size, LANES) for k in range(2)], axis=1
        )
        high, low = halves(right)
        total = jnp.dot(
            left, jnp.concatenate([high, low], axis=0), preferred_element_type=jnp.float32
        )
        total = total[:size] + total[size:]
        for k in range(2):
            out_ref[:, x + k] = total[:, k * LANES : (k + 1) * LANES].reshape(
                size // block, block, LANES
            )


def solver_kernel(*refs):
    n = len(CHUNKS)
    code_ref, *rest = refs
    f_refs, out_refs = rest[:n], rest[n : 2 * n]
    v_ref, w_ref, d_ref, f1_ref, v1_ref, w1_ref, d1_ref = rest[2 * n :]
    modes = v_ref.shape[2]
    shape = (modes, LANES)
    lane = lax.broadcasted_iota(jnp.int32, shape, 1)
    mode = lax.broadcasted_iota(jnp.int32, shape, 0)
    zero = jnp.zeros(shape, jnp.float32)
    code = jnp.zeros(shape, jnp.int32)
    for m in range(modes):
        code = jnp.where(mode == m, code_ref[m], code)
    shift = 0.05 * jnp.exp2(code.astype(jnp.float32) / 4.0)
    group = lax.axis_index("gx")
    left = ROBIN * (group > 0).astype(jnp.float32)
    right = ROBIN * (group < lax.axis_size("gx") - 1).astype(jnp.float32)

    def edge_of(x, count):
        return (left if x == 0 else 0.0) + (right if x == count - 1 else 0.0)

    for x in range(PLANES):
        if x in (0, PLANES - 1) or x == 1:
            diag = shift + (6.0 + edge_of(x, PLANES))
            weight = DAMPING / diag
        d_ref[x] = diag
        w_ref[x] = weight
    for x in range(PLANES // 2):
        if x in (0, PLANES // 2 - 1) or x == 1:
            diag = shift + 0.25 * (6.0 + edge_of(x, PLANES // 2))
            weight = DAMPING / diag
        d1_ref[x] = diag
        w1_ref[x] = weight

    segments = []
    for f_ref, out_ref, starts in zip(f_refs, out_refs, CHUNKS):
        for i, start in enumerate(starts):
            segments.append((start, i, f_ref, out_ref))
    segments.sort(key=lambda s: s[0])

    roll = lambda value, by: pltpu.roll(value, by % LANES, 1)
    low_half = lane < 64
    y_first = lane % 64 == 0
    y_last = lane % 64 == 63

    def neighbours(before, here, after):
        turned = [roll(v, 64) for v in here]
        sums = []
        for c in range(TILES):
            total = before[c] + after[c] + turned[c]
            down = turned[c - 1] if c > 0 else zero
            up = turned[c + 1] if c < TILES - 1 else zero
            total = total + jnp.where(low_half, down, up)
            total = total + jnp.where(y_first, zero, roll(here[c], 1))
            total = total + jnp.where(y_last, zero, roll(here[c], -1))
            sums.append(total)
        return sums

    def march(plane_at, work, unroll):
        carry = [zero] * TILES, plane_at(0, 0, 0)
        for s in range(len(segments)):
            last = s == len(segments) - 1

            def body(step, carry, s=s, last=last, final=False):
                before, here = carry
                window = [before, here]
                for u in range(unroll):
                    x = step * unroll + u + 1
                    if final and u == unroll - 1:
                        window.append([zero] * TILES if last else plane_at(s + 1, 0, 0))
                    else:
                        window.append(plane_at(s, x, u + 1))
                work(s, step * unroll, window)
                return window[-2], window[-1]

            carry = lax.fori_loop(0, DEPTH // unroll - 1, body, carry)
            carry = body(DEPTH // unroll - 1, carry, final=True)

    def right_side(s, x):
        _, i, f_ref, _ = segments[s]
        return [f_ref[i * TILES + c, x] for c in range(TILES)]

    def field(s, x, u):
        start = segments[s][0]
        return [v_ref[start + x, c * modes // modes] if False else v_ref[start + x, c] for c in range(TILES)]

    def scaled(s, x, u):
        start = segments[s][0]
        weight = w_ref[start + x]
        return [weight * f for f in right_side(s, x)]

    def corrected(s, x, u):
        start = segments[s][0]
        coarse = v1_ref[(start + x) // 2]
        return [
            v_ref[start + x, c]
            + jnp.take_along_axis(coarse, c * 32 + lane % 64 // 2, axis=1)
            for c in range(TILES)
        ]

    def sweep(final):
        def work(s, x, window):
            start, i, _, out_ref = segments[s]
            for u in range(len(window) - 2):
                before, here, after = window[u : u + 3]
                weight = w_ref[start + x + u]
                sums = neighbours(before, here, after)
                f = right_side(s, x + u)
                for c in range(TILES):
                    value = (1.0 - DAMPING) * here[c] + weight * (f[c] + sums[c])
                    if final:
                        out_ref[i * TILES + c, x + u] = value
                    else:
                        v_ref[start + x + u, c] = value

        return work

    def residual(s, x, window):
        start = segments[s][0]
        planes = []
        for u in range(len(window) - 2):
            before, here, after = window[u : u + 3]
            diag = d_ref[start + x + u]
            sums = neighbours(before, here, after)
            f = right_side(s, x + u)
            planes.append([f[c] - (diag * here[c] - sums[c]) for c in range(TILES)])
        for u in range(0, len(planes), 2):
            pair = [planes[u][c] + planes[u + 1][c] for c in range(TILES)]
            parts = []
            for c in (0, 2):
                both = jnp.where(low_half, pair[c], pair[c + 1]) + roll(
                    jnp.where(low_half, pair[c + 1], pair[c]), 64
                )
                both = both + roll(both, -1)
                parts.append(
                    jnp.take_along_axis(both, lane % 64 // 32 * 64 + lane % 32 * 2, axis=1)
                )
            f1_ref[(start + x + u) // 2] = 0.125 * jnp.where(low_half, parts[0], parts[1])

    z_first = lane < 32
    z_last = lane >= 96
    y1_first = lane % 32 == 0
    y1_last = lane % 32 == 31
    half = PLANES // 2

    def neighbours1(before, here, after):
        total = before + after
        total = total + jnp.where(z_first, zero, roll(here, 32))
        total = total + jnp.where(z_last, zero, roll(here, -32))
        total = total + jnp.where(y1_first, zero, roll(here, 1))
        return total + jnp.where(y1_last, zero, roll(here, -1))

    def march1(plane_at, work):
        before, here = zero, plane_at(0)
        for x in range(half):
            after = plane_at(x + 1) if x + 1 < half else zero
            work(x, before, here, after)
            before, here = here, after

    def sweep1(x, before, here, after):
        total = f1_ref[x] + 0.25 * neighbours1(before, here, after)
        v1_ref[x] = (1.0 - DAMPING) * here + w1_ref[x] * total

    used = lane < 32
    quarter = half // 2
    y2_first = lane % 16 == 0
    y2_last = lane % 16 == 15

    def coarsest(f2):
        weights = []
        for x in range(quarter):
            if x in (0, quarter - 1) or x == 1:
                diag = shift + 0.0625 * (6.0 + edge_of(x, quarter))
                weight = jnp.where(used, DAMPING / diag, zero)
            weights.append(weight)
        g = [weights[x] * f2[x] for x in range(quarter)]
        v = g
        for _ in range(5):
            new = []
            for x in range(quarter):
                total = (v[x - 1] if x > 0 else zero) + (v[x + 1] if x < quarter - 1 else zero)
                total = total + roll(v[x], 16) + roll(v[x], -16)
                total = total + jnp.where(y2_first, zero, roll(v[x], 1))
                total = total + jnp.where(y2_last, zero, roll(v[x], -1))
                new.append((1.0 - DAMPING) * v[x] + g[x] + (0.0625 * weights[x]) * total)
            v = new
        return v

    def level1():
        march1(lambda x: w1_ref[x] * f1_ref[x], sweep1)
        r1 = [None] * half

        def residual1(x, before, here, after):
            r1[x] = f1_ref[x] - (d1_ref[x] * here - 0.25 * neighbours1(before, here, after))

        march1(lambda x: v1_ref[x], residual1)
        f2 = []
        for x in range(quarter):
            pair = r1[2 * x] + r1[2 * x + 1]
            pair = pair + roll(pair, -32)
            pair = pair + roll(pair, -1)
            picked = jnp.take_along_axis(pair, lane % 32 // 16 * 64 + lane % 16 * 2, axis=1)
            f2.append(jnp.where(used, 0.125 * picked, zero))
        v2 = coarsest(f2)
        spread = [
            jnp.take_along_axis(v, lane // 64 * 16 + lane % 32 // 2, axis=1) for v in v2
        ]
        march1(lambda x: v1_ref[x] + spread[x // 2], sweep1)
        march1(lambda x: v1_ref[x], sweep1)

    for cycle in range(CYCLES):
        if cycle == 0:
            march(scaled, sweep(False), UNROLL)
        else:
            march(field, sweep(False), UNROLL)
            march(field, sweep(False), UNROLL)
        march(field, residual, UNROLL)
        level1()
        march(corrected, sweep(False), UNROLL)
        march(field, sweep(cycle == CYCLES - 1), UNROLL)


def vmem(count):
    return [pl.BlockSpec(memory_space=pltpu.VMEM)] * count


def body(source, previous, time_modes, time_back, step_code):
    steps = source.shape[0]
    peers = lax.axis_size("ta")
    count = lax.axis_size("gx")
    first, last = previous[:, 0, :], previous[:, PLANES - 1, :]
    forward = [(i, i + 1) for i in range(count - 1)]
    low = lax.ppermute(last, "gx", forward)
    high = lax.ppermute(first, "gx", [(b, a) for a, b in forward])
    shape = jax.ShapeDtypeStruct((peers, DEPTH, steps, LANES), jnp.float32)
    flat = jax.ShapeDtypeStruct((peers * DEPTH * steps, LANES), jnp.float32)

    def exchange(value):
        return lax.all_to_all(value, "ta", split_axis=0, concat_axis=0, tiled=True)

    def product(matrix, value):
        return pl.pallas_call(
            product_kernel, out_shape=shape, in_specs=vmem(2), out_specs=vmem(1)[0]
        )(matrix, value)

    modes = []
    for starts in CHUNKS:
        edges = 0 in starts
        extra = (low, high, first, last) if edges else ()
        packed = pl.pallas_call(
            functools.partial(pack_kernel, starts, edges),
            out_shape=flat,
            in_specs=vmem(1 + len(extra)),
            out_specs=vmem(1)[0],
        )(source, *extra)
        modes.append(exchange(product(time_modes, exchange(packed.reshape(shape.shape)))))
    n = len(CHUNKS)
    solved = pl.pallas_call(
        solver_kernel,
        out_shape=[shape] * n,
        in_specs=[pl.BlockSpec(memory_space=pltpu.SMEM)] + vmem(n),
        out_specs=vmem(n),
        scratch_shapes=[
            pltpu.VMEM((PLANES, TILES, steps, LANES), jnp.float32),
            pltpu.VMEM((PLANES, steps, LANES), jnp.float32),
            pltpu.VMEM((PLANES, steps, LANES), jnp.float32),
            pltpu.VMEM((PLANES // 2, steps, LANES), jnp.float32),
            pltpu.VMEM((PLANES // 2, steps, LANES), jnp.float32),
            pltpu.VMEM((PLANES // 2, steps, LANES), jnp.float32),
            pltpu.VMEM((PLANES // 2, steps, LANES), jnp.float32),
        ],
    )(step_code, *modes)
    back = [exchange(product(time_back, exchange(value))).reshape(flat.shape) for value in solved]
    return pl.pallas_call(
        unpack_kernel,
        out_shape=jax.ShapeDtypeStruct(source.shape, jnp.float32),
        in_specs=vmem(n),
        out_specs=vmem(1)[0],
    )(*back)


def solution(mesh):
    placed = (P("ta", "gx", None), P("ta", "gx", None), P(), P(), P("ta"))
    return jax.shard_map(
        body, mesh=mesh, in_specs=placed, out_specs=P("ta", "gx", None), check_vma=False
    )
```

time: 206 us -> 128 us (0.62); the launches traced: 203 us -> 127 us
  local copies, waits for them, and re-layouts: 61.8 us -> 1.71 us
  other arithmetic: 36.3 us -> 0 us
  Pallas kernels: 0 us -> 33.5 us
  blocking collectives: 55.9 us -> 81 us
  waiting for transfers between devices: 22.3 us -> 1.56 us
  matrix products: 14 us -> 0 us
  starting transfers between devices: 11.6 us -> 9.46 us
    pallas_call x0 -> x5, Pallas kernels: none -> 33.5 us  [the longest x1 23.1 us: body(): pl.pallas_call(solver_kernel, out_shape=[shape] * n, in_specs=[pl.BlockSp...]
    all_to_all x3 -> x4, blocking collectives: 55.9 us -> 81 us  [exchange(): return lax.all_to_all(value, 'ta', split_axis=0, concat_axis=0, tiled=True)]
    unnamed x20 -> x10, local copies, waits for them, and re-layouts: 23.4 us -> 0.63 us
    all_to_all x2 -> x0, waiting for transfers between devices: 15.4 us -> none  [several_exchanges(): lax.all_to_all(section, axis, split_axis=0, concat_axis=0, tiled=True)]
    dot_general x10 -> x0, matrix products: 14 us -> none  [the longest x1 4.15 us: body(): jnp.einsum('mt,txc->mxc', time_modes, lax.all_to_all(rhs, 'ta', split_axi...]
    all_to_all x5 -> x0, other arithmetic: 13 us -> none  [the longest x2 3.71 us: several_exchanges(): lax.all_to_all(section, axis, split_axis=0, concat_axis=0, tiled=True)]
    all_to_all x5 -> x0, local copies, waits for them, and re-layouts: 12.3 us -> none  [the longest x2 5.66 us: body(): return lax.all_to_all(mixed, 'ta', split_axis=0, concat_axis=2, tiled=True)]
    add x25 -> x0, other arithmetic: 10.4 us -> none  [the longest x18 9.94 us: smooth(): field = field + DAMPING * (target - applied) / diag]
  transfers between devices with their start and end apart: 4 -> 2, of which waited for: 4 -> 1; matrix products, arithmetic and copies ran while one was open for 3% -> 0% of each run, Pallas kernels for 0% -> 0%
where the time goes in v1:
time: 128 us; the launch traced here: 127 us
  blocking collectives  81 us (63%)
  Pallas kernels  33.5 us (26%)
  starting transfers between devices  9.46 us (7%)
  local copies, waits for them, and re-layouts  1.71 us (1%)
  waiting for transfers between devices  1.56 us (1%)
    all_to_all x4, blocking collectives, exchange(): return lax.all_to_all(value, 'ta', split_axis=0, concat_axis=0, tiled=True)  81 us
    pallas_call x1, Pallas kernels, body(): pl.pallas_call(solver_kernel, out_shape=[shape] * n, in_specs=[pl.BlockSp...  23.1 us
    ppermute x1, starting transfers between devices, body(): high = lax.ppermute(first, 'gx', [(b, a) for a, b in forward])  7.53 us
    pallas_call x2, Pallas kernels, product(): pl.pallas_call(product_kernel, out_shape=shape, in_specs=vmem(2), out_spe...  5.35 us
    pallas_call x1, Pallas kernels, body(): pl.pallas_call(functools.partial(pack_kernel, starts, edges), out_shape=f...  2.58 us
  transfers between devices with their start and end apart: 2, of which 1 were waited for; matrix products, arithmetic and copies ran while one was open for 0% of the time, Pallas kernels for 0%

profile of v1, /device:TPU:16, one launch (start us, length us, event | category | flops | bytes accessed | tf_op | source)
XLA Modules:
  0.0 127.3 jit_solution(2603962854117694402)
XLA Ops:
  0.0 1.1 fusion
  1.1 0.0 copy-start
  1.1 1.9 %collective-permute-start = (f32[16,512]{1,0:T(8,128)S(1)}, f32[16,512]{1,0:T(8,128)S(1)}, u32[]{:S(2)}, u32[]{:S(2)}) collective-permute-start(f32[16,512]{1,0:T(8,128)S(1)} %bitcast.10), channel_id=1, source_target_pairs={{0,8},{8,16},{16,24},{24,32},{32,40},{40,48},{48,56},{56,64},{64,7... | collective-permute-start | bytes 98312 | tf_op jit(solution)/shard_map/ppermute | solution.py:326
  3.0 0.0 copy-done
  3.1 0.0 copy-start.1
  3.1 7.5 %collective-permute-start.1 = (f32[16,512]{1,0:T(8,128)S(1)}, f32[16,512]{1,0:T(8,128)S(1)}, u32[]{:S(2)}, u32[]{:S(2)}) collective-permute-start(f32[16,512]{1,0:T(8,128)S(1)} %bitcast.12), channel_id=1, source_target_pairs={{8,0},{16,8},{24,16},{32,24},{40,32},{48,40},{56,48},{64,56},{72,6... | collective-permute-start | bytes 98312 | tf_op jit(solution)/shard_map/ppermute | solution.py:327
  10.6 0.0 collective-permute-done.refs_1_
  10.6 0.0 copy-start.2
  10.6 1.6 %collective-permute-done.1.refs_2_ = f32[16,512]{1,0:T(8,128)S(1)} collective-permute-done((f32[16,512]{1,0:T(8,128)S(1)}, f32[16,512]{1,0:T(8,128)S(1)}, u32[]{:S(2)}, u32[]{:S(2)}) %collective-permute-start.1) | collective-permute-done | bytes 32800 | tf_op jit(solution)/shard_map/ppermute | solution.py:327
  12.2 0.0 copy-done.1
  12.2 0.0 copy-done.2
  12.2 0.0 copy-start.3
  12.2 0.6 copy-done.3
  12.8 2.6 %shard_map.55 = f32[2048,128]{1,0:T(8,128)} custom-call(f32[16,32,512]{2,1,0:T(8,128)} %refs_0_.2, f32[16,512]{1,0:T(8,128)} %copy-done.2, f32[16,512]{1,0:T(8,128)} %copy-done.3, f32[16,512]{1,0:T(8,128)} %bitcast.13, f32[16,512]{1,0:T(8,128)} %bitcast.11), custom_call_target="tpu_custom_call" | custom-call | tf_op jit(solution)/shard_map/pallas_call | solution.py:343
  15.4 22.1 %all_to_all.20.in_ref = f32[8,16,16,128]{3,2,1,0:T(8,128)} all-to-all(f32[8,16,16,128]{3,2,1,0:T(8,128)} %bitcast.8), channel_id=1, replica_groups=mesh['gx'=32,'ta'=8] {'ta'}, dimensions={0} | all-to-all | bytes 2097152 | tf_op jit(solution)/shard_map/all_to_all | solution.py:332
  37.5 2.7 %shard_map.56 = f32[8,16,16,128]{3,2,1,0:T(8,128)} custom-call(f32[128,128]{1,0:T(8,128)} %matrix_ref.2, f32[8,16,16,128]{3,2,1,0:T(8,128)} %all_to_all.20.in_ref), custom_call_target="tpu_custom_call" | custom-call | tf_op jit(solution)/shard_map/pallas_call | solution.py:335
  40.1 20.5 %all_to_all.21.refs_1_ = f32[8,16,16,128]{3,2,1,0:T(8,128)} all-to-all(f32[8,16,16,128]{3,2,1,0:T(8,128)} %shard_map.56), channel_id=1, replica_groups=mesh['gx'=32,'ta'=8] {'ta'}, dimensions={0} | all-to-all | bytes 2097152 | tf_op jit(solution)/shard_map/all_to_all | solution.py:332
  60.6 23.1 %shard_map.57 = f32[8,16,16,128]{3,2,1,0:T(8,128)} custom-call(s32[16]{0:T(128)} %refs_0_.3, f32[8,16,16,128]{3,2,1,0:T(8,128)} %all_to_all.21.refs_1_), custom_call_target="tpu_custom_call" | custom-call | tf_op jit(solution)/shard_map/pallas_call | solution.py:351
  83.7 19.6 %all_to_all.22.in_ref = f32[8,16,16,128]{3,2,1,0:T(8,128)} all-to-all(f32[8,16,16,128]{3,2,1,0:T(8,128)} %shard_map.57), channel_id=1, replica_groups=mesh['gx'=32,'ta'=8] {'ta'}, dimensions={0} | all-to-all | bytes 2097152 | tf_op jit(solution)/shard_map/all_to_all | solution.py:332
  103.3 2.7 %shard_map.58 = f32[8,16,16,128]{3,2,1,0:T(8,128)} custom-call(f32[128,128]{1,0:T(8,128)} %matrix_ref.3, f32[8,16,16,128]{3,2,1,0:T(8,128)} %all_to_all.22.in_ref), custom_call_target="tpu_custom_call" | custom-call | tf_op jit(solution)/shard_map/pallas_call | solution.py:335
  106.0 18.8 %all_to_all.23 = f32[8,16,16,128]{3,2,1,0:T(8,128)} all-to-all(f32[8,16,16,128]{3,2,1,0:T(8,128)} %shard_map.58), channel_id=1, replica_groups=mesh['gx'=32,'ta'=8] {'ta'}, dimensions={0} | all-to-all | bytes 2097152 | tf_op jit(solution)/shard_map/all_to_all | solution.py:332
  124.8 2.5 %shard_map.59 = f32[16,32,512]{2,1,0:T(8,128)} custom-call(f32[2048,128]{1,0:T(8,128)} %bitcast.9), custom_call_target="tpu_custom_call" | custom-call | tf_op jit(solution)/shard_map/pallas_call | solution.py:367
  (2 shorter events, 0.0 us)
Async XLA Ops:
  1.1 2.0 %copy-start = (f32[16,1,512]{2,0,1:T(8,128)}, f32[16,1,512]{2,0,1:T(8,128)S(1)}, u32[]{:S(2)}) copy-start(f32[16,1,512]{2,0,1:T(8,128)S(1)} %copy.13) | copy-start | bytes 98308
  1.1 9.5 %collective-permute-start = (f32[16,512]{1,0:T(8,128)S(1)}, f32[16,512]{1,0:T(8,128)S(1)}, u32[]{:S(2)}, u32[]{:S(2)}) collective-permute-start(f32[16,512]{1,0:T(8,128)S(1)} %bitcast.10), channel_id=1, source_target_pairs={{0,8},{8,16},{16,24},{24,32},{32,40},{40,48},{48,56},{56,64},{64,7... | collective-permute-start | bytes 98312 | tf_op jit(solution)/shard_map/ppermute | solution.py:326
  3.1 9.1 %copy-start.1 = (f32[16,1,512]{2,0,1:T(8,128)}, f32[16,1,512]{2,0,1:T(8,128)S(1)}, u32[]{:S(2)}) copy-start(f32[16,1,512]{2,0,1:T(8,128)S(1)} %copy.12) | copy-start | bytes 98308
  3.1 9.1 %collective-permute-start.1 = (f32[16,512]{1,0:T(8,128)S(1)}, f32[16,512]{1,0:T(8,128)S(1)}, u32[]{:S(2)}, u32[]{:S(2)}) collective-permute-start(f32[16,512]{1,0:T(8,128)S(1)} %bitcast.12), channel_id=1, source_target_pairs={{8,0},{16,8},{24,16},{32,24},{40,32},{48,40},{56,48},{64,56},{72,6... | collective-permute-start | bytes 98312 | tf_op jit(solution)/shard_map/ppermute | solution.py:327
  10.6 1.6 %copy-start.2 = (f32[16,512]{1,0:T(8,128)}, f32[16,512]{1,0:T(8,128)S(1)}, u32[]{:S(2)}) copy-start(f32[16,512]{1,0:T(8,128)S(1)} %collective-permute-done.refs_1_) | copy-start | bytes 98308
  12.2 0.6 copy-start.3

commit v2 on v0

v2 whole, which is shorter than its diff:
```python
import functools

import jax
import jax.numpy as jnp
from jax import lax
from jax.experimental import pallas as pl
from jax.experimental.pallas import tpu as pltpu
from jax.sharding import PartitionSpec as P

CYCLES = 2
ROBIN = 1.0
DAMPING = 0.8
LANES = 128
SIDE = 8
HIGH = 8
LOW = 4
CZ = 8
CY = 64
TILES = 4
GROUP = 2
LIMIT = 24 * 2**20


def params():
    return pltpu.CompilerParams(vmem_limit_bytes=LIMIT)


def pack_kernel(source_ref, low_ref, high_ref, first_ref, last_ref, out_ref, turned_ref):
    steps = source_ref.shape[0]
    planes = HIGH * LOW
    for tile in range(TILES):
        cells = pl.ds(tile * LANES, LANES)
        for t in range(steps):
            for row in range(0, planes, 8):
                turned_ref[pl.ds((tile * planes + row) * steps + t, 8, stride=steps), :] = source_ref[
                    t, pl.ds(row, 8), cells
                ]
    group = lax.axis_index("gx")
    left = (group > 0).astype(jnp.float32)
    right = (group < lax.axis_size("gx") - 1).astype(jnp.float32)
    for half in range(2):
        for tile in range(TILES):
            cells = pl.ds(tile * LANES, LANES)
            for low in range(2):
                for high in range(HIGH):
                    x = high * LOW + 2 * half + low
                    value = turned_ref[pl.ds((tile * planes + x) * steps, steps), :]
                    if x == 0:
                        value += left * (low_ref[:, cells] - ROBIN * first_ref[:, cells])
                    if x == planes - 1:
                        value += right * (high_ref[:, cells] - ROBIN * last_ref[:, cells])
                    out_ref[half * TILES + tile, low * HIGH + high] = value


def unpack_kernel(in_ref, out_ref, turned_ref):
    steps = out_ref.shape[0]
    planes = HIGH * LOW
    for half in range(2):
        for tile in range(TILES):
            for low in range(2):
                for high in range(HIGH):
                    x = high * LOW + 2 * half + low
                    turned_ref[pl.ds((tile * planes + x) * steps, steps), :] = in_ref[
                        half * TILES + tile, low * HIGH + high
                    ]
    for tile in range(TILES):
        for t in range(steps):
            for row in range(0, planes, 8):
                out_ref[t, pl.ds(row, 8), pl.ds(tile * LANES, LANES)] = turned_ref[
                    pl.ds((tile * planes + row) * steps + t, 8, stride=steps), :
                ]


def halves(value):
    high = value.astype(jnp.bfloat16)
    return high, (value - high.astype(jnp.float32)).astype(jnp.bfloat16)


def regroup(values):
    block = lax.broadcasted_iota(jnp.int32, values[0].shape, 1) // (LANES // SIDE)
    values = [values[-q % SIDE] for q in range(SIDE)]
    for bit in (1, 2, 4):
        odd = (block & bit) != 0
        values = [jnp.where(odd, values[(q - bit) % SIDE], values[q]) for q in range(SIDE)]
    return values


def forward_kernel(matrix_ref, in_ref, out_ref, mixed_ref):
    size = matrix_ref.shape[0]
    matrix = matrix_ref[...].T
    for high in range(HIGH):
        turned = pltpu.roll(matrix, high * (LANES // SIDE), 1) if high else matrix
        main, rest = halves(turned)
        right = jnp.concatenate([main, rest], axis=1)
        right = jnp.concatenate([right, right], axis=0)
        parts = [in_ref[:, low * HIGH + high].reshape(size, LANES).T for low in range(2)]
        main, rest = halves(jnp.concatenate(parts, axis=0))
        total = jnp.dot(
            jnp.concatenate([main, rest], axis=1), right, preferred_element_type=jnp.float32
        )
        mixed_ref[high] = total[:, :size] + total[:, size:]
    for row in range(0, 2 * LANES, 8):
        rows = pl.ds(row, 8)
        for owner, value in enumerate(regroup([mixed_ref[high, rows, :] for high in range(HIGH)])):
            out_ref[owner, rows, :] = value


def backward_kernel(matrix_ref, in_ref, out_ref, mixed_ref):
    size = matrix_ref.shape[0]
    block = out_ref.shape[2]
    for row in range(0, 2 * LANES, 8):
        rows = pl.ds(row, 8)
        for high, value in enumerate(regroup([in_ref[owner, rows, :] for owner in range(SIDE)])):
            mixed_ref[high, rows, :] = value
    matrix = matrix_ref[...]
    for high in range(HIGH):
        turned = pltpu.roll(matrix, high * (LANES // SIDE), 1) if high else matrix
        main, rest = halves(turned)
        left = jnp.concatenate(
            [jnp.concatenate([main, main], axis=1), jnp.concatenate([rest, rest], axis=1)], axis=0
        )
        main, rest = halves(mixed_ref[high])
        total = lax.dot_general(
            left,
            jnp.concatenate([main, rest], axis=1),
            (((1,), (1,)), ((), ())),
            preferred_element_type=jnp.float32,
        )
        total = total[:size] + total[size:]
        for low in range(2):
            out_ref[:, low * HIGH + high] = total[:, low * LANES : (low + 1) * LANES].reshape(
                size // block, block, LANES
            )


def solver_kernel(code_ref, f_ref, out_ref, *scratch):
    va, vb, spread_ref, f1_ref, v1a, v1b, spread1_ref, f2_ref, v2a, v2b = scratch
    shape = (8, LANES)
    lane = lax.broadcasted_iota(jnp.int32, shape, 1)
    modes = LANES // SIDE
    zero = jnp.zeros(shape, jnp.float32)
    code = jnp.zeros(shape, jnp.int32)
    for m in range(modes):
        code = jnp.where(lane % modes == m, code_ref[m], code)
    shift = 0.05 * jnp.exp2(code.astype(jnp.float32) / 4.0)
    group = lax.axis_index("gx")
    has_left = ROBIN * (group > 0).astype(jnp.float32)
    has_right = ROBIN * (group < lax.axis_size("gx") - 1).astype(jnp.float32)
    high = (lane // modes - lax.axis_index("ta") + SIDE) % SIDE
    x_first = high == 0
    x_last = high == SIDE - 1
    left = jnp.where(x_first, has_left, zero)
    right = jnp.where(x_last, has_right, zero)

    class Level:
        def __init__(self, level, field, other, right_side, low, cz, cy):
            self.scale = 0.25**level
            self.fields = (field, other)
            self.right_side = right_side
            self.low, self.cz, self.cy = low, cz, cy
            self.pitch = cy + 8
            self.diag, self.weight = [], []
            for x in range(low):
                edge = 6.0 + (left if x == 0 else zero)
                if x == low - 1:
                    edge = edge + right
                self.diag.append(shift + self.scale * edge)
                self.weight.append(DAMPING / self.diag[-1])
            for ref in self.fields:
                for k in range(low * cz + 1):
                    ref[pl.ds(k * self.pitch, 8), :] = zero

        def base(self, x, z):
            return 8 + (x * self.cz + z) * self.pitch

        def load(self, ref, x, z, row):
            return ref[pl.ds(self.base(x, z) + row, 8), :]

        def store(self, ref, x, z, row, value):
            ref[pl.ds(self.base(x, z) + row, 8), :] = value

        def sums(self, ref, row):
            here = [[self.load(ref, x, z, row) for z in range(self.cz)] for x in range(self.low)]
            step = LANES // SIDE
            wrap_low = [pltpu.roll(here[-1][z], step, 1) for z in range(self.cz)]
            wrap_high = [pltpu.roll(here[0][z], LANES - step, 1) for z in range(self.cz)]
            for x in range(self.low):
                for z in range(self.cz):
                    total = self.load(ref, x, z, row - 1) + self.load(ref, x, z, row + 1)
                    if z > 0:
                        total = total + here[x][z - 1]
                    if z < self.cz - 1:
                        total = total + here[x][z + 1]
                    if x > 0:
                        total = total + here[x - 1][z]
                    if x < self.low - 1:
                        total = total + here[x + 1][z]
                    if x == 0:
                        total = total + jnp.where(x_first, zero, wrap_low[z])
                    if x == self.low - 1:
                        total = total + jnp.where(x_last, zero, wrap_high[z])
                    if self.scale != 1.0:
                        total = self.scale * total
                    yield x, z, here[x][z], total

        def over_rows(self, work):
            size = min(8 * GROUP, self.cy)
            if size == self.cy:
                for row in range(0, size, 8):
                    work(row)
                return

            def body(step, carry):
                for k in range(0, size, 8):
                    work(pl.multiple_of(step * size, 8) + k)
                return carry

            lax.fori_loop(0, self.cy // size, body, 0)

        def start(self, ref):
            def work(row):
                for x in range(self.low):
                    for z in range(self.cz):
                        self.store(ref, x, z, row, self.weight[x] * self.right_side(x, z, row))

            self.over_rows(work)

        def sweep(self, source, target=None, emit=None):
            def work(row):
                for x, z, here, total in self.sums(source, row):
                    f = self.right_side(x, z, row)
                    value = (1.0 - DAMPING) * here + self.weight[x] * (f + total)
                    if emit is None:
                        self.store(target, x, z, row, value)
                    else:
                        emit(x, z, row, value)

            self.over_rows(work)

        def residual(self, ref, spread, coarse_f):
            def work(row):
                parts = {}
                for x, z, here, total in self.sums(ref, row):
                    f = self.right_side(x, z, row)
                    value = f - (self.diag[x] * here - total)
                    key = (x // 2, z // 2)
                    parts[key] = parts[key] + value if key in parts else value
                for (x, z), value in parts.items():
                    spread[pl.ds((x * (self.cz // 2) + z) * self.cy + row, 8), :] = value

            self.over_rows(work)
            for k in range(max(self.low // 2, 1) * self.cz // 2):
                for row in range(0, self.cy // 2, 8):
                    start = k * self.cy + 2 * row
                    coarse_f[pl.ds(k * (self.cy // 2) + row, 8), :] = 0.125 * (
                        spread[pl.ds(start, 8, stride=2), :]
                        + spread[pl.ds(start + 1, 8, stride=2), :]
                    )

        def correct(self, ref, spread, coarse, coarse_ref):
            for x in range(coarse.low):
                for z in range(coarse.cz):
                    for row in range(0, coarse.cy, 8):
                        value = coarse.load(coarse_ref, x, z, row)
                        start = (x * coarse.cz + z) * self.cy + 2 * row
                        spread[pl.ds(start, 8, stride=2), :] = value
                        spread[pl.ds(start + 1, 8, stride=2), :] = value

            def work(row):
                for x in range(self.low):
                    for z in range(self.cz):
                        k = (x * coarse.low // self.low) * coarse.cz + z // 2
                        value = spread[pl.ds(k * self.cy + row, 8), :]
                        self.store(ref, x, z, row, self.load(ref, x, z, row) + value)

            self.over_rows(work)

    def fine_rows(x, z, row):
        return (x // 2) * TILES + z // 2, pl.ds((x % 2) * LANES + (z % 2) * CY + row, 8)

    def fine_f(x, z, row):
        peer, rows = fine_rows(x, z, row)
        return f_ref[peer, rows, :]

    def emit(x, z, row, value):
        peer, rows = fine_rows(x, z, row)
        out_ref[peer, rows, :] = value

    def coarse_f(ref, cz, cy):
        return lambda x, z, row: ref[pl.ds((x * cz + z) * cy + row, 8), :]

    fine = Level(0, va, vb, fine_f, LOW, CZ, CY)
    middle = Level(1, v1a, v1b, coarse_f(f1_ref, CZ // 2, CY // 2), LOW // 2, CZ // 2, CY // 2)
    coarse = Level(2, v2a, v2b, coarse_f(f2_ref, CZ // 4, CY // 4), 1, CZ // 4, CY // 4)

    for cycle in range(CYCLES):
        if cycle == 0:
            fine.start(vb)
            fine.sweep(vb, va)
        else:
            fine.sweep(va, vb)
            fine.sweep(vb, va)
        fine.residual(va, spread_ref, f1_ref)
        middle.start(v1b)
        middle.sweep(v1b, v1a)
        middle.residual(v1a, spread1_ref, f2_ref)
        coarse.start(v2a)
        for _ in range(2):
            coarse.sweep(v2a, v2b)
            coarse.sweep(v2b, v2a)
        coarse.sweep(v2a, v2b)
        middle.correct(v1a, spread1_ref, coarse, v2b)
        middle.sweep(v1a, v1b)
        middle.sweep(v1b, v1a)
        fine.correct(va, spread_ref, middle, v1a)
        fine.sweep(va, vb)
        if cycle == CYCLES - 1:
            fine.sweep(vb, emit=emit)
        else:
            fine.sweep(vb, va)


def vmem(count):
    return [pl.BlockSpec(memory_space=pltpu.VMEM)] * count


def rows(count):
    return pltpu.VMEM((count, LANES), jnp.float32)


def body(source, previous, time_modes, time_back, step_code):
    steps, planes, _ = source.shape
    peers = lax.axis_size("ta")
    count = lax.axis_size("gx")
    first, last = previous[:, 0, :], previous[:, planes - 1, :]
    forward = [(i, i + 1) for i in range(count - 1)]
    low = lax.ppermute(last, "gx", forward)
    high = lax.ppermute(first, "gx", [(b, a) for a, b in forward])
    by_step = jax.ShapeDtypeStruct((peers, planes // 2, steps, LANES), jnp.float32)
    by_mode = jax.ShapeDtypeStruct((peers, 2 * LANES, LANES), jnp.float32)
    mixed = pltpu.VMEM((HIGH, 2 * LANES, LANES), jnp.float32)
    turned = rows(TILES * planes * steps)

    def exchange(value):
        return lax.all_to_all(value, "ta", split_axis=0, concat_axis=0, tiled=True)

    def call(kernel, shape, count, *scratch):
        return pl.pallas_call(
            kernel,
            out_shape=shape,
            in_specs=vmem(count),
            out_specs=vmem(1)[0],
            scratch_shapes=scratch,
            compiler_params=params(),
        )

    packed = call(pack_kernel, by_step, 5, turned)(source, low, high, first, last)
    modes = exchange(call(forward_kernel, by_mode, 2, mixed)(time_modes, exchange(packed)))
    solved = pl.pallas_call(
        solver_kernel,
        out_shape=by_mode,
        in_specs=[pl.BlockSpec(memory_space=pltpu.SMEM)] + vmem(1),
        out_specs=vmem(1)[0],
        scratch_shapes=[
            *[rows(8 + LOW * CZ * (CY + 8))] * 2,
            rows(LOW * CZ // 4 * CY),
            rows(LOW * CZ // 4 * CY // 2),
            *[rows(8 + LOW * CZ // 4 * (CY // 2 + 8))] * 2,
            rows(CZ // 4 * CY // 2),
            rows(CZ // 4 * CY // 4),
            *[rows(8 + CZ // 4 * (CY // 4 + 8))] * 2,
        ],
        compiler_params=params(),
    )(step_code, modes)
    mixed_back = call(backward_kernel, by_step, 2, mixed)(time_back, exchange(solved))
    out = jax.ShapeDtypeStruct(source.shape, jnp.float32)
    return call(unpack_kernel, out, 1, turned)(exchange(mixed_back))


def solution(mesh):
    placed = (P("ta", "gx", None), P("ta", "gx", None), P(), P(), P("ta"))
    return jax.shard_map(
        body, mesh=mesh, in_specs=placed, out_specs=P("ta", "gx", None), check_vma=False
    )
```

time: 206 us -> 100 us (0.49); the launches traced: 203 us -> 99.6 us
  local copies, waits for them, and re-layouts: 61.8 us -> 2.33 us
  other arithmetic: 36.3 us -> 0 us
  waiting for transfers between devices: 22.3 us -> 1.57 us
  blocking collectives: 55.9 us -> 75.7 us
  matrix products: 14 us -> 0 us
  Pallas kernels: 0 us -> 10.5 us
  starting transfers between devices: 11.6 us -> 9.46 us
    unnamed x20 -> x10, local copies, waits for them, and re-layouts: 23.4 us -> 1.25 us
    all_to_all x3 -> x4, blocking collectives: 55.9 us -> 75.7 us  [exchange(): return lax.all_to_all(value, 'ta', split_axis=0, concat_axis=0, tiled=True)]
    all_to_all x2 -> x0, waiting for transfers between devices: 15.4 us -> none  [several_exchanges(): lax.all_to_all(section, axis, split_axis=0, concat_axis=0, tiled=True)]
    dot_general x10 -> x0, matrix products: 14 us -> none  [the longest x1 4.15 us: body(): jnp.einsum('mt,txc->mxc', time_modes, lax.all_to_all(rhs, 'ta', split_axi...]
    all_to_all x5 -> x0, other arithmetic: 13 us -> none  [the longest x2 3.71 us: several_exchanges(): lax.all_to_all(section, axis, split_axis=0, concat_axis=0, tiled=True)]
    all_to_all x5 -> x0, local copies, waits for them, and re-layouts: 12.3 us -> none  [the longest x2 5.66 us: body(): return lax.all_to_all(mixed, 'ta', split_axis=0, concat_axis=2, tiled=True)]
    pallas_call x0 -> x5, Pallas kernels: none -> 10.5 us  [the longest x1 7.39 us: body(): pl.pallas_call(solver_kernel, out_shape=by_mode, in_specs=[pl.BlockSpec(m...]
    add x25 -> x0, other arithmetic: 10.4 us -> none  [the longest x18 9.94 us: smooth(): field = field + DAMPING * (target - applied) / diag]
  transfers between devices with their start and end apart: 4 -> 2, of which waited for: 4 -> 1; matrix products, arithmetic and copies ran while one was open for 3% -> 0% of each run, Pallas kernels for 0% -> 0%
where the time goes in v2:
time: 100 us; the launch traced here: 99.6 us
  blocking collectives  75.7 us (76%)
  Pallas kernels  10.5 us (10%)
  starting transfers between devices  9.46 us (9%)
  local copies, waits for them, and re-layouts  2.33 us (2%)
  waiting for transfers between devices  1.57 us (2%)
    all_to_all x4, blocking collectives, exchange(): return lax.all_to_all(value, 'ta', split_axis=0, concat_axis=0, tiled=True)  75.7 us
    ppermute x1, starting transfers between devices, body(): high = lax.ppermute(first, 'gx', [(b, a) for a, b in forward])  7.53 us
    pallas_call x1, Pallas kernels, body(): pl.pallas_call(solver_kernel, out_shape=by_mode, in_specs=[pl.BlockSpec(m...  7.39 us
  transfers between devices with their start and end apart: 2, of which 1 were waited for; matrix products, arithmetic and copies ran while one was open for 0% of the time, Pallas kernels for 0%

profile of v2, /device:TPU:16, one launch (start us, length us, event | category | flops | bytes accessed | tf_op | source)
XLA Modules:
  0.0 99.6 jit_solution(13201935338270561779)
XLA Ops:
  0.0 1.1 %fusion = (f32[16,1,512]{2,1,0:T(1,128)S(1)}, f32[16,1,512]{2,1,0:T(1,128)S(1)}) fusion(f32[16,32,512]{2,1,0:T(8,128)} %param.6), kind=kLoop, calls=%fused_computation.2 | loop fusion | bytes 131072 | tf_op jit(solution)/shard_map/slice | solution.py:335
  1.1 1.9 %collective-permute-start = (f32[16,512]{1,0:T(8,128)S(1)}, f32[16,512]{1,0:T(8,128)S(1)}, u32[]{:S(2)}, u32[]{:S(2)}) collective-permute-start(f32[16,512]{1,0:T(8,128)S(1)} %bitcast.6), channel_id=1, source_target_pairs={{0,8},{8,16},{16,24},{24,32},{32,40},{40,48},{48,56},{56,64},{64,7... | collective-permute-start | bytes 98312 | tf_op jit(solution)/shard_map/ppermute | solution.py:337
  3.0 7.5 %collective-permute-start.1 = (f32[16,512]{1,0:T(8,128)S(1)}, f32[16,512]{1,0:T(8,128)S(1)}, u32[]{:S(2)}, u32[]{:S(2)}) collective-permute-start(f32[16,512]{1,0:T(8,128)S(1)} %bitcast.8), channel_id=1, source_target_pairs={{8,0},{16,8},{24,16},{32,24},{40,32},{48,40},{56,48},{64,56},{72,6... | collective-permute-start | bytes 98312 | tf_op jit(solution)/shard_map/ppermute | solution.py:338
  10.6 0.0 collective-permute-done.low_ref
  10.6 1.6 %collective-permute-done.1.high_ref = f32[16,512]{1,0:T(8,128)S(1)} collective-permute-done((f32[16,512]{1,0:T(8,128)S(1)}, f32[16,512]{1,0:T(8,128)S(1)}, u32[]{:S(2)}, u32[]{:S(2)}) %collective-permute-start.1) | collective-permute-done | bytes 32800 | tf_op jit(solution)/shard_map/ppermute | solution.py:338
  12.2 0.0 copy-start
  12.2 1.2 %copy-done = f32[16,32,512]{2,1,0:T(8,128)S(1)} copy-done((f32[16,32,512]{2,1,0:T(8,128)S(1)}, f32[16,32,512]{2,1,0:T(8,128)}, u32[]{:S(2)}) %copy-start) | copy-done | bytes 1048600
  13.4 0.5 shard_map.55
  13.9 0.0 copy-start.1
  13.9 21.9 %all_to_all.20.in_ref = f32[8,16,16,128]{3,2,1,0:T(8,128)S(1)} all-to-all(f32[8,16,16,128]{3,2,1,0:T(8,128)S(1)} %shard_map.55), channel_id=1, replica_groups=mesh['gx'=32,'ta'=8] {'ta'}, dimensions={0} | all-to-all | bytes 2097152 | tf_op jit(solution)/shard_map/all_to_all | solution.py:345
  35.8 0.0 copy-done.1
  35.8 0.7 shard_map.56
  36.6 0.0 copy-start.3
  36.6 18.7 %all_to_all.21.f_ref = f32[8,256,128]{2,1,0:T(8,128)S(1)} all-to-all(f32[8,256,128]{2,1,0:T(8,128)S(1)} %shard_map.56), channel_id=1, replica_groups=mesh['gx'=32,'ta'=8] {'ta'}, dimensions={0} | all-to-all | bytes 2097152 | tf_op jit(solution)/shard_map/all_to_all | solution.py:345
  55.2 0.0 copy-done.3
  55.3 7.4 %shard_map.57 = f32[8,256,128]{2,1,0:T(8,128)S(1)} custom-call(s32[16]{0:T(128)S(1)} %copy-done.3, f32[8,256,128]{2,1,0:T(8,128)S(1)} %all_to_all.21.f_ref), custom_call_target="tpu_custom_call" | custom-call | tf_op jit(solution)/shard_map/pallas_call | solution.py:359
  62.6 0.0 copy-start.2
  62.7 17.9 %all_to_all.22.in_ref = f32[8,256,128]{2,1,0:T(8,128)S(1)} all-to-all(f32[8,256,128]{2,1,0:T(8,128)S(1)} %shard_map.57), channel_id=1, replica_groups=mesh['gx'=32,'ta'=8] {'ta'}, dimensions={0} | all-to-all | bytes 2097152 | tf_op jit(solution)/shard_map/all_to_all | solution.py:345
  80.6 0.0 copy-done.2
  80.6 0.5 shard_map.58
  81.1 17.1 %all_to_all.23.in_ref = f32[8,16,16,128]{3,2,1,0:T(8,128)S(1)} all-to-all(f32[8,16,16,128]{3,2,1,0:T(8,128)S(1)} %shard_map.58), channel_id=1, replica_groups=mesh['gx'=32,'ta'=8] {'ta'}, dimensions={0} | all-to-all | bytes 2097152 | tf_op jit(solution)/shard_map/all_to_all | solution.py:345
  98.3 1.4 %shard_map.59 = f32[16,32,512]{2,1,0:T(8,128)} custom-call(f32[8,16,16,128]{3,2,1,0:T(8,128)S(1)} %all_to_all.23.in_ref), custom_call_target="tpu_custom_call" | custom-call | tf_op jit(solution)/shard_map/pallas_call | solution.py:377
  (2 shorter events, 0.0 us)
Async XLA Ops:
  1.1 9.5 %collective-permute-start = (f32[16,512]{1,0:T(8,128)S(1)}, f32[16,512]{1,0:T(8,128)S(1)}, u32[]{:S(2)}, u32[]{:S(2)}) collective-permute-start(f32[16,512]{1,0:T(8,128)S(1)} %bitcast.6), channel_id=1, source_target_pairs={{0,8},{8,16},{16,24},{24,32},{32,40},{40,48},{48,56},{56,64},{64,7... | collective-permute-start | bytes 98312 | tf_op jit(solution)/shard_map/ppermute | solution.py:337
  3.0 9.1 %collective-permute-start.1 = (f32[16,512]{1,0:T(8,128)S(1)}, f32[16,512]{1,0:T(8,128)S(1)}, u32[]{:S(2)}, u32[]{:S(2)}) collective-permute-start(f32[16,512]{1,0:T(8,128)S(1)} %bitcast.8), channel_id=1, source_target_pairs={{8,0},{16,8},{24,16},{32,24},{40,32},{48,40},{56,48},{64,56},{72,6... | collective-permute-start | bytes 98312 | tf_op jit(solution)/shard_map/ppermute | solution.py:338
  12.2 1.2 %copy-start = (f32[16,32,512]{2,1,0:T(8,128)S(1)}, f32[16,32,512]{2,1,0:T(8,128)}, u32[]{:S(2)}) copy-start(f32[16,32,512]{2,1,0:T(8,128)} %source_ref.1) | copy-start | bytes 3145732
  13.9 21.9 %copy-start.1 = (f32[128,128]{1,0:T(8,128)S(1)}, f32[128,128]{1,0:T(8,128)}, u32[]{:S(2)}) copy-start(f32[128,128]{1,0:T(8,128)} %matrix_ref.2) | copy-start | bytes 196612
  36.6 18.7 %copy-start.3 = (s32[16]{0:T(128)S(1)}, s32[16]{0:T(128)}, u32[]{:S(2)}) copy-start(s32[16]{0:T(128)} %code_ref.1) | copy-start | bytes 196
  62.6 17.9 %copy-start.2 = (f32[128,128]{1,0:T(8,128)S(1)}, f32[128,128]{1,0:T(8,128)}, u32[]{:S(2)}) copy-start(f32[128,128]{1,0:T(8,128)} %matrix_ref.3) | copy-start | bytes 196612

commit v3 on v2

--- a/solution.py
+++ b/solution.py
@@ -1,11 +1,10 @@
-import functools
-
 import jax
 import jax.numpy as jnp
 from jax import lax
 from jax.experimental import pallas as pl
 from jax.experimental.pallas import tpu as pltpu
 from jax.sharding import PartitionSpec as P
+
 
 CYCLES = 2
 ROBIN = 1.0
@@ -17,17 +16,21 @@
 CZ = 8
 CY = 64
 TILES = 4
-GROUP = 2
+GROUP = 4
 LIMIT = 24 * 2**20
-
-
-def params():
-    return pltpu.CompilerParams(vmem_limit_bytes=LIMIT)
-
-
-def pack_kernel(source_ref, low_ref, high_ref, first_ref, last_ref, out_ref, turned_ref):
+PAUSE = 1800
+
+
+def has_neighbours():
+    group = lax.axis_index("gx")
+    left = (group > 0).astype(jnp.float32)
+    return left, (group < lax.axis_size("gx") - 1).astype(jnp.float32)
+
+
+def turn_kernel(source_ref, first_ref, last_ref, turned_ref):
     steps = source_ref.shape[0]
     planes = HIGH * LOW
+    left, right = has_neighbours()
     for tile in range(TILES):
         cells = pl.ds(tile * LANES, LANES)
         for t in range(steps):
@@ -35,21 +38,34 @@
                 turned_ref[pl.ds((tile * planes + row) * steps + t, 8, stride=steps), :] = source_ref[
                     t, pl.ds(row, 8), cells
                 ]
-    group = lax.axis_index("gx")
-    left = (group > 0).astype(jnp.float32)
-    right = (group < lax.axis_size("gx") - 1).astype(jnp.float32)
+        turned_ref[pl.ds(tile * planes * steps, steps), :] -= (left * ROBIN) * first_ref[:, cells]
+        turned_ref[pl.ds((tile * planes + planes - 1) * steps, steps), :] -= (
+            right * ROBIN
+        ) * last_ref[:, cells]
+
+
+def pack_kernel(turned_ref, outer_ref, inner_ref, out_ref, pause_ref):
+    steps = out_ref.shape[2]
+    planes = HIGH * LOW
+    left, right = has_neighbours()
+    odd = lax.axis_index("gx") % 2 == 1
     for half in range(2):
         for tile in range(TILES):
             cells = pl.ds(tile * LANES, LANES)
+            outer, inner = outer_ref[:, cells], inner_ref[:, cells]
             for low in range(2):
                 for high in range(HIGH):
                     x = high * LOW + 2 * half + low
                     value = turned_ref[pl.ds((tile * planes + x) * steps, steps), :]
                     if x == 0:
-                        value += left * (low_ref[:, cells] - ROBIN * first_ref[:, cells])
+                        value += left * jnp.where(odd, inner, outer)
                     if x == planes - 1:
-                        value += right * (high_ref[:, cells] - ROBIN * last_ref[:, cells])
+                        value += right * jnp.where(odd, outer, inner)
                     out_ref[half * TILES + tile, low * HIGH + high] = value
+    late = lax.axis_index("gx") % 2
+    pause_ref[...] = lax.fori_loop(
+        0, late * PAUSE, lambda _, value: pltpu.roll(value, 1, 1), out_ref[0, 0, :8, :]
+    )
 
 
 def unpack_kernel(in_ref, out_ref, turned_ref):
@@ -143,9 +159,7 @@
     for m in range(modes):
         code = jnp.where(lane % modes == m, code_ref[m], code)
     shift = 0.05 * jnp.exp2(code.astype(jnp.float32) / 4.0)
-    group = lax.axis_index("gx")
-    has_left = ROBIN * (group > 0).astype(jnp.float32)
-    has_right = ROBIN * (group < lax.axis_size("gx") - 1).astype(jnp.float32)
+    has_left, has_right = (ROBIN * side for side in has_neighbours())
     high = (lane // modes - lax.axis_index("ta") + SIDE) % SIDE
     x_first = high == 0
     x_last = high == SIDE - 1
@@ -204,7 +218,7 @@
                     yield x, z, here[x][z], total
 
         def over_rows(self, work):
-            size = min(8 * GROUP, self.cy)
+            size = min(8 * GROUP, self.cy) if self.scale == 1.0 else self.cy
             if size == self.cy:
                 for row in range(0, size, 8):
                     work(row)
@@ -328,57 +342,65 @@
     return pltpu.VMEM((count, LANES), jnp.float32)
 
 
-def body(source, previous, time_modes, time_back, step_code):
+def exchange(value):
+    return lax.all_to_all(value, "ta", split_axis=0, concat_axis=0, tiled=True)
+
+
+def swaps(start, count):
+    pairs = [(i, i + 1) for i in range(start, count - 1, 2)]
+    return pairs + [(b, a) for a, b in pairs]
+
+
+def call(kernel, shape, count, *scratch, smem=0, flops=10**6):
+    return pl.pallas_call(
+        kernel,
+        out_shape=shape,
+        in_specs=[pl.BlockSpec(memory_space=pltpu.SMEM)] * smem + vmem(count),
+        out_specs=vmem(1)[0],
+        scratch_shapes=scratch,
+        compiler_params=pltpu.CompilerParams(vmem_limit_bytes=LIMIT),
+        cost_estimate=pl.CostEstimate(flops=flops, bytes_accessed=2**20, transcendentals=0),
+    )
+
+
+def iteration(source, previous, time_modes, time_back, step_code):
     steps, planes, _ = source.shape
-    peers = lax.axis_size("ta")
     count = lax.axis_size("gx")
     first, last = previous[:, 0, :], previous[:, planes - 1, :]
-    forward = [(i, i + 1) for i in range(count - 1)]
-    low = lax.ppermute(last, "gx", forward)
-    high = lax.ppermute(first, "gx", [(b, a) for a, b in forward])
-    by_step = jax.ShapeDtypeStruct((peers, planes // 2, steps, LANES), jnp.float32)
-    by_mode = jax.ShapeDtypeStruct((peers, 2 * LANES, LANES), jnp.float32)
-    mixed = pltpu.VMEM((HIGH, 2 * LANES, LANES), jnp.float32)
-    turned = rows(TILES * planes * steps)
-
-    def exchange(value):
-        return lax.all_to_all(value, "ta", split_axis=0, concat_axis=0, tiled=True)
-
-    def call(kernel, shape, count, *scratch):
-        return pl.pallas_call(
-            kernel,
-            out_shape=shape,
-            in_specs=vmem(count),
-            out_specs=vmem(1)[0],
-            scratch_shapes=scratch,
-            compiler_params=params(),
-        )
-
-    packed = call(pack_kernel, by_step, 5, turned)(source, low, high, first, last)
-    modes = exchange(call(forward_kernel, by_mode, 2, mixed)(time_modes, exchange(packed)))
-    solved = pl.pallas_call(
+    odd = lax.axis_index("gx") % 2 == 1
+    outer = lax.ppermute(jnp.where(odd, last, first), "gx", swaps(1, count))
+    outer, inner = lax.optimization_barrier((outer, jnp.where(odd, first, last)))
+    inner = lax.ppermute(inner, "gx", swaps(0, count))
+    by_step = jax.ShapeDtypeStruct((SIDE, planes // 2, steps, LANES), jnp.float32)
+    by_mode = jax.ShapeDtypeStruct((SIDE, 2 * LANES, LANES), jnp.float32)
+    turned = (TILES * planes * steps, LANES)
+    blocks = pltpu.VMEM((SIDE, 2 * LANES, LANES), jnp.float32)
+
+    held = call(turn_kernel, jax.ShapeDtypeStruct(turned, jnp.float32), 3, flops=10**8)(
+        source, first, last
+    )
+    packed = call(pack_kernel, by_step, 3, rows(8))(held, outer, inner)
+    mixed = call(forward_kernel, by_mode, 2, blocks)(time_modes, exchange(packed))
+    solved = call(
         solver_kernel,
-        out_shape=by_mode,
-        in_specs=[pl.BlockSpec(memory_space=pltpu.SMEM)] + vmem(1),
-        out_specs=vmem(1)[0],
-        scratch_shapes=[
-            *[rows(8 + LOW * CZ * (CY + 8))] * 2,
-            rows(LOW * CZ // 4 * CY),
-            rows(LOW * CZ // 4 * CY // 2),
-            *[rows(8 + LOW * CZ // 4 * (CY // 2 + 8))] * 2,
-            rows(CZ // 4 * CY // 2),
-            rows(CZ // 4 * CY // 4),
-            *[rows(8 + CZ // 4 * (CY // 4 + 8))] * 2,
-        ],
-        compiler_params=params(),
-    )(step_code, modes)
-    mixed_back = call(backward_kernel, by_step, 2, mixed)(time_back, exchange(solved))
-    out = jax.ShapeDtypeStruct(source.shape, jnp.float32)
-    return call(unpack_kernel, out, 1, turned)(exchange(mixed_back))
+        by_mode,
+        1,
+        *[rows(8 + LOW * CZ * (CY + 8))] * 2,
+        rows(LOW * CZ // 4 * CY),
+        rows(LOW * CZ // 4 * CY // 2),
+        *[rows(8 + LOW * CZ // 4 * (CY // 2 + 8))] * 2,
+        rows(CZ // 4 * CY // 2),
+        rows(CZ // 4 * CY // 4),
+        *[rows(8 + CZ // 4 * (CY // 4 + 8))] * 2,
+        smem=1,
+    )(step_code, exchange(mixed))
+    mixed = call(backward_kernel, by_step, 2, blocks)(time_back, exchange(solved))
+    result = jax.ShapeDtypeStruct(source.shape, jnp.float32)
+    return call(unpack_kernel, result, 1, rows(turned[0]))(exchange(mixed))
 
 
 def solution(mesh):
     placed = (P("ta", "gx", None), P("ta", "gx", None), P(), P(), P("ta"))
     return jax.shard_map(
-        body, mesh=mesh, in_specs=placed, out_specs=P("ta", "gx", None), check_vma=False
+        iteration, mesh=mesh, in_specs=placed, out_specs=P("ta", "gx", None), check_vma=False
     )

time: 100 us -> 86 us (0.86)
  the two profiles are of different devices: /device:TPU:16 before, /device:TPU:25 now
where the time goes in v3:
time: 86 us; the launch traced here: 85.6 us
  blocking collectives  54.2 us (63%)
  Pallas kernels  18.9 us (22%)
  starting transfers between devices  8.5 us (10%)
  local copies, waits for them, and re-layouts  2.33 us (3%)
  waiting for transfers between devices  1.59 us (2%)
    all_to_all x4, blocking collectives, exchange(): return lax.all_to_all(value, 'ta', split_axis=0, concat_axis=0, tiled=True)  54.2 us
    pallas_call x1, Pallas kernels, iteration(): packed = call(pack_kernel, by_step, 3, rows(8))(held, outer, inner)  9.55 us
    pallas_call x1, Pallas kernels, iteration(): call(solver_kernel, by_mode, 1, *[rows(8 + LOW * CZ * (CY + 8))] * 2, row...  6.3 us
    ppermute x1, starting transfers between devices, iteration(): outer = lax.ppermute(jnp.where(odd, last, first), 'gx', swaps(1, count))  5.46 us
    ppermute x1, starting transfers between devices, iteration(): inner = lax.ppermute(inner, 'gx', swaps(0, count))  3.04 us
  transfers between devices with their start and end apart: 2, of which 1 were waited for; matrix products, arithmetic and copies ran while one was open for 0% of the time, Pallas kernels for 1%

profile of v3, /device:TPU:25, one launch (start us, length us, event | category | flops | bytes accessed | tf_op | source)
XLA Modules:
  0.0 85.6 jit_solution(14420264613964645440)
XLA Ops:
  0.0 1.1 %fusion = (f32[16,1,512]{2,1,0:T(1,128)S(1)}, f32[16,1,512]{2,1,0:T(1,128)S(1)}) fusion(f32[16,32,512]{2,1,0:T(8,128)} %param.6), kind=kLoop, calls=%fused_computation.4 | loop fusion | bytes 131072 | tf_op jit(solution)/shard_map/slice | solution.py:369
  1.1 5.5 %collective-permute-start = (f32[16,512]{1,0:T(8,128)S(1)}, f32[16,512]{1,0:T(8,128)S(1)}, u32[]{:S(2)}, u32[]{:S(2)}) collective-permute-start(f32[16,512]{1,0:T(8,128)S(1)} %get-tuple-element.12), channel_id=1, source_target_pairs={{8,16},{24,32},{40,48},{56,64},{72,80},{88,96},{104,112},{120,128}... | collective-permute-start | bytes 98312 | tf_op jit(solution)/shard_map/ppermute | solution.py:371
  6.6 1.6 %collective-permute-done.outer_ref = f32[16,512]{1,0:T(8,128)S(1)} collective-permute-done((f32[16,512]{1,0:T(8,128)S(1)}, f32[16,512]{1,0:T(8,128)S(1)}, u32[]{:S(2)}, u32[]{:S(2)}) %collective-permute-start) | collective-permute-done | bytes 32800 | tf_op jit(solution)/shard_map/ppermute | solution.py:371
  8.2 3.0 %collective-permute-start.1 = (f32[16,512]{1,0:T(8,128)S(1)}, f32[16,512]{1,0:T(8,128)S(1)}, u32[]{:S(2)}, u32[]{:S(2)}) collective-permute-start(f32[16,512]{1,0:T(8,128)S(1)} %get-tuple-element.8), channel_id=1, source_target_pairs={{0,8},{16,24},{32,40},{48,56},{64,72},{80,88},{96,104},{112,120},{... | collective-permute-start | bytes 98312 | tf_op jit(solution)/shard_map/ppermute | solution.py:373
  11.2 0.0 copy-start
  11.2 1.2 %copy-done = f32[16,32,512]{2,1,0:T(8,128)S(1)} copy-done((f32[16,32,512]{2,1,0:T(8,128)S(1)}, f32[16,32,512]{2,1,0:T(8,128)}, u32[]{:S(2)}) %copy-start) | copy-done | bytes 1048600
  12.4 0.4 shard_map.55.turned_ref
  12.9 0.0 collective-permute-done.1.inner_ref
  12.9 9.5 %shard_map.56 = f32[8,16,16,128]{3,2,1,0:T(8,128)S(1)} custom-call(f32[2048,128]{1,0:T(8,128)S(1)} %shard_map.55.turned_ref, f32[16,512]{1,0:T(8,128)S(1)} %collective-permute-done.outer_ref, f32[16,512]{1,0:T(8,128)S(1)} %collective-permute-done.1.inner_ref), custom_call_target="tpu_custom_call" | custom-call | flops 1000000 | bytes 1048576 | tf_op jit(solution)/shard_map/pallas_call | solution.py:382
  22.4 0.0 copy-start.1
  22.5 14.8 %all_to_all.20.in_ref = f32[8,16,16,128]{3,2,1,0:T(8,128)S(1)} all-to-all(f32[8,16,16,128]{3,2,1,0:T(8,128)S(1)} %shard_map.56), channel_id=1, replica_groups=mesh['gx'=32,'ta'=8] {'ta'}, dimensions={0} | all-to-all | bytes 2097152 | tf_op jit(solution)/shard_map/all_to_all | solution.py:346
  37.2 0.0 copy-done.1
  37.2 0.7 shard_map.57
  37.9 0.0 copy-start.3
  38.0 12.8 %all_to_all.21.f_ref = f32[8,256,128]{2,1,0:T(8,128)S(1)} all-to-all(f32[8,256,128]{2,1,0:T(8,128)S(1)} %shard_map.57), channel_id=1, replica_groups=mesh['gx'=32,'ta'=8] {'ta'}, dimensions={0} | all-to-all | bytes 2097152 | tf_op jit(solution)/shard_map/all_to_all | solution.py:346
  50.7 0.0 copy-done.3
  50.7 6.3 %shard_map.58 = f32[8,256,128]{2,1,0:T(8,128)S(1)} custom-call(s32[16]{0:T(128)S(1)} %copy-done.3, f32[8,256,128]{2,1,0:T(8,128)S(1)} %all_to_all.21.f_ref), custom_call_target="tpu_custom_call" | custom-call | flops 1000000 | bytes 1048576 | tf_op jit(solution)/shard_map/pallas_call | solution.py:384
  57.0 0.0 copy-start.2
  57.0 12.9 %all_to_all.22.in_ref = f32[8,256,128]{2,1,0:T(8,128)S(1)} all-to-all(f32[8,256,128]{2,1,0:T(8,128)S(1)} %shard_map.58), channel_id=1, replica_groups=mesh['gx'=32,'ta'=8] {'ta'}, dimensions={0} | all-to-all | bytes 2097152 | tf_op jit(solution)/shard_map/all_to_all | solution.py:346
  69.9 0.0 copy-done.2
  70.0 0.5 shard_map.59
  70.5 13.8 %all_to_all.23.in_ref = f32[8,16,16,128]{3,2,1,0:T(8,128)S(1)} all-to-all(f32[8,16,16,128]{3,2,1,0:T(8,128)S(1)} %shard_map.59), channel_id=1, replica_groups=mesh['gx'=32,'ta'=8] {'ta'}, dimensions={0} | all-to-all | bytes 2097152 | tf_op jit(solution)/shard_map/all_to_all | solution.py:346
  84.3 1.4 %shard_map.60 = f32[16,32,512]{2,1,0:T(8,128)} custom-call(f32[8,16,16,128]{3,2,1,0:T(8,128)S(1)} %all_to_all.23.in_ref), custom_call_target="tpu_custom_call" | custom-call | flops 1000000 | bytes 1048576 | tf_op jit(solution)/shard_map/pallas_call | solution.py:399
  (2 shorter events, 0.0 us)
Async XLA Ops:
  1.1 7.1 %collective-permute-start = (f32[16,512]{1,0:T(8,128)S(1)}, f32[16,512]{1,0:T(8,128)S(1)}, u32[]{:S(2)}, u32[]{:S(2)}) collective-permute-start(f32[16,512]{1,0:T(8,128)S(1)} %get-tuple-element.12), channel_id=1, source_target_pairs={{8,16},{24,32},{40,48},{56,64},{72,80},{88,96},{104,112},{120,128}... | collective-permute-start | bytes 98312 | tf_op jit(solution)/shard_map/ppermute | solution.py:371
  8.2 4.7 %collective-permute-start.1 = (f32[16,512]{1,0:T(8,128)S(1)}, f32[16,512]{1,0:T(8,128)S(1)}, u32[]{:S(2)}, u32[]{:S(2)}) collective-permute-start(f32[16,512]{1,0:T(8,128)S(1)} %get-tuple-element.8), channel_id=1, source_target_pairs={{0,8},{16,24},{32,40},{48,56},{64,72},{80,88},{96,104},{112,120},{... | collective-permute-start | bytes 98312 | tf_op jit(solution)/shard_map/ppermute | solution.py:373
  11.2 1.2 %copy-start = (f32[16,32,512]{2,1,0:T(8,128)S(1)}, f32[16,32,512]{2,1,0:T(8,128)}, u32[]{:S(2)}) copy-start(f32[16,32,512]{2,1,0:T(8,128)} %source_ref.1) | copy-start | bytes 3145732
  22.4 14.8 %copy-start.1 = (f32[128,128]{1,0:T(8,128)S(1)}, f32[128,128]{1,0:T(8,128)}, u32[]{:S(2)}) copy-start(f32[128,128]{1,0:T(8,128)} %matrix_ref.2) | copy-start | bytes 196612
  37.9 12.8 %copy-start.3 = (s32[16]{0:T(128)S(1)}, s32[16]{0:T(128)}, u32[]{:S(2)}) copy-start(s32[16]{0:T(128)} %code_ref.1) | copy-start | bytes 196
  57.0 12.9 %copy-start.2 = (f32[128,128]{1,0:T(8,128)S(1)}, f32[128,128]{1,0:T(8,128)}, u32[]{:S(2)}) copy-start(f32[128,128]{1,0:T(8,128)} %matrix_ref.3) | copy-start | bytes 196612
